TPU v7x, 32 devices: a whole 2x2x4 slice. The times are simulated.
32 devices in a mesh: rows: 16 (over z, y, x), cols: 2 (over core).
Axes of the slice: x: 2, y: 2, z: 4, core: 2. Of those that a mesh axis runs over, the one named last changes fastest.
Arguments:
- eigvecs: float32 [4096, 2048], P('rows', 'cols'), may hold values from -6 to 6
- reflectors: float32 [32, 4096], P('cols', 'rows'), may hold values from -17 to 17
- starts: int32 [32], replicated, may hold values from 0 to 63
Outputs:
- rotated: float32 [4096, 2048], P('rows', 'cols')
Inputs may be any that keep to these rules, and one draw needn't show every extreme that they name: Sweep j's windows begin at rows starts[j] + k * 64.
All inputs are finite; a program needn't handle non-finite values.
Results may differ from a plain program's by a relative error of at most 0.00011.
Values sent between devices are 32-bit elements; how exact they have to be, the bound alone decides.
A program may use at most 64 MiB of HBM per device.

v0:
```python
import jax
import jax.numpy as jnp
from jax import lax
from jax.sharding import PartitionSpec as P

BAND = 64
SWEEPS = 32


def column_sweep(turned, reflector, offset):
    width = turned.shape[0]
    total_rows = turned.shape[1]
    blocks = total_rows // BAND
    rolled = jnp.roll(turned, -offset, axis=1).reshape(width, blocks, BAND)
    rolled_v = jnp.roll(reflector, -offset).reshape(blocks, BAND)
    squares = jnp.sum(rolled_v * rolled_v, axis=1)
    window = jnp.arange(blocks, dtype=jnp.int32)
    usable = (window + 1) * BAND + offset <= total_rows
    scaled = jnp.where(usable, 2.0 / jnp.where(usable, squares, 1.0), 0.0)
    products = jnp.sum(rolled * rolled_v[None, :, :], axis=2)
    rolled = rolled - (products * scaled[None, :])[:, :, None] * rolled_v[None, :, :]
    return jnp.roll(rolled.reshape(width, total_rows), offset, axis=1)


def per_device(eigvecs, reflectors, starts):
    every_sweep = lax.all_gather(reflectors, "cols", axis=0, tiled=True)
    turned = lax.all_to_all(eigvecs, "rows", split_axis=1, concat_axis=0, tiled=True)
    whole_v = lax.all_gather(every_sweep, "rows", axis=1, tiled=True)
    crossed = turned.T

    def advance(sweep_idx, state):
        return column_sweep(state, whole_v[sweep_idx], starts[sweep_idx])

    crossed = lax.fori_loop(0, SWEEPS, advance, crossed)
    return lax.all_to_all(crossed.T, "rows", split_axis=0, concat_axis=1, tiled=True)


def solution(mesh):
    in_specs = (P("rows", "cols"), P("cols", "rows"), P())
    out_specs = P("rows", "cols")
    return jax.shard_map(
        per_device, mesh=mesh, in_specs=in_specs, out_specs=out_specs, check_vma=False
    )
```

profile of v0, /device:TPU:12, one launch (start us, length us, event | category | flops | bytes accessed | tf_op | source)
XLA Modules:
  0.0 525.6 jit_solution(18121734052208252811)
XLA Ops:
  0.0 2.5 copy.12
  2.5 7.3 %all-to-all-start = ((f32[256,16,64]{0,2,1:T(8,128)}), f32[256,16,64]{0,2,1:T(8,128)S(1)}, u32[]{:S(2)}, u32[]{:S(2)}) async-start(f32[256,16,64]{0,2,1:T(8,128)} %bitcast.2), calls=%async_computation | async-start | bytes 2097152 | tf_op jit(solution)/shard_map/all_to_all | solution.py:27
  11.7 51.4 %all_gather.7 = f32[32,4096]{1,0:T(8,128)} all-gather(f32[32,256]{1,0:T(8,128)S(1)} %all_gather.6), channel_id=1, replica_groups=mesh['rows'=16,'cols'=2] {'rows'}, dimensions={1}, use_global_device_ids=true | all-gather | bytes 557056 | tf_op jit(solution)/shard_map/all_gather | solution.py:28
  63.2 435.8 %while.15 = (s32[]{:T(128)}, f32[64,4096]{1,0:T(8,128)S(1)}, s32[32]{0:T(128)S(1)}, f32[32,4096]{1,0:T(8,128)}, s32[]{:T(128)}, /*index=5*/s32[]{:T(128)}, s32[]{:T(128)}, s32[]{:T(128)}, s32[]{:T(128)}) while((s32[]{:T(128)}, f32[64,4096]{1,0:T(8,128)S(1)}, s32[32]{0:T(128)S(1)}, f32[32,4096]{1,0:T(8,128)}, s32[]{:T(128)}, ...), condition=%wide.region_3.5_spmd, body=%wide.region_0.4_spmd.sunk | while | flops 1847711 | bytes 13845943 | solution.py:34
  67.6 2.0 reshape.75
  74.3 1.8 multiply_subtract_fusion.2
  81.3 2.0 reshape.75
  87.9 1.8 multiply_subtract_fusion.2
  94.9 2.0 reshape.75
  101.5 1.8 multiply_subtract_fusion.2
  108.5 2.0 reshape.75
  115.2 1.8 multiply_subtract_fusion.2
  122.1 2.0 reshape.75
  128.8 1.8 multiply_subtract_fusion.2
  135.7 2.0 reshape.75
  142.4 1.8 multiply_subtract_fusion.2
  149.4 2.0 reshape.75
  156.0 1.8 multiply_subtract_fusion.2
  163.0 2.0 reshape.75
  169.6 1.8 multiply_subtract_fusion.2
  176.6 2.0 reshape.75
  183.3 1.8 multiply_subtract_fusion.2
  190.2 2.0 reshape.75
  196.9 1.8 multiply_subtract_fusion.2
  203.8 2.0 reshape.75
  210.5 1.8 multiply_subtract_fusion.2
  217.5 2.0 reshape.75
  224.1 1.8 multiply_subtract_fusion.2
  231.1 2.0 reshape.75
  237.7 1.8 multiply_subtract_fusion.2
  244.7 2.0 reshape.75
  251.4 1.8 multiply_subtract_fusion.2
  258.3 2.0 reshape.75
  265.0 1.8 multiply_subtract_fusion.2
  271.9 2.0 reshape.75
  278.6 1.8 multiply_subtract_fusion.2
  285.6 2.0 reshape.75
  292.2 1.8 multiply_subtract_fusion.2
  299.2 2.0 reshape.75
  305.8 1.8 multiply_subtract_fusion.2
  312.8 2.0 reshape.75
  319.5 1.8 multiply_subtract_fusion.2
  326.4 2.0 reshape.75
  333.1 1.8 multiply_subtract_fusion.2
  340.0 2.0 reshape.75
  346.7 1.8 multiply_subtract_fusion.2
  353.6 2.0 reshape.75
  360.3 1.8 multiply_subtract_fusion.2
  367.3 2.0 reshape.75
  373.9 1.8 multiply_subtract_fusion.2
  380.9 2.0 reshape.75
  387.6 1.8 multiply_subtract_fusion.2
  394.5 2.0 reshape.75
  401.2 1.8 multiply_subtract_fusion.2
  408.1 2.0 reshape.75
  421.7 2.0 reshape.75
  428.4 1.8 multiply_subtract_fusion.2
  435.4 2.0 reshape.75
  449.0 2.0 reshape.75
  462.6 2.0 reshape.75
  469.3 1.8 multiply_subtract_fusion.2
  476.2 2.0 reshape.75
  489.8 2.0 reshape.75
  499.1 25.2 %all_to_all.38 = f32[16,256,64]{1,2,0:T(8,128)S(1)} all-to-all(f32[16,256,64]{1,2,0:T(8,128)S(1)} %bitcast.23), channel_id=1, replica_groups=mesh['rows'=16,'cols'=2] {'rows'}, dimensions={0} | all-to-all | bytes 2097152 | tf_op jit(solution)/shard_map/all_to_all | solution.py:35
  (398 shorter events, 249.9 us)
Async XLA Ops:
  0.0 9.8 %copy-start = (f32[16,256]{1,0:T(8,128)S(1)}, f32[16,256]{1,0:T(8,128)}, u32[]{:S(2)}) copy-start(f32[16,256]{1,0:T(8,128)} %param.8) | copy-start | bytes 49156
  2.5 60.6 %copy-start.1 = (s32[32]{0:T(128)S(1)}, s32[32]{0:T(128)}, u32[]{:S(2)}) copy-start(s32[32]{0:T(128)} %param.9) | copy-start | bytes 388
  2.5 60.5 %all-to-all-start = ((f32[256,16,64]{0,2,1:T(8,128)}), f32[256,16,64]{0,2,1:T(8,128)S(1)}, u32[]{:S(2)}, u32[]{:S(2)}) async-start(f32[256,16,64]{0,2,1:T(8,128)} %bitcast.2), calls=%async_computation | async-start | bytes 2097152 | tf_op jit(solution)/shard_map/all_to_all | solution.py:27
where the time goes:
time: 532 us; the launch traced here: 526 us
  local copies, waits for them, and re-layouts  190 us (36%)
  other arithmetic  174 us (33%)
  blocking collectives  78.4 us (15%)
  loops' own time  75.8 us (14%)
  starting transfers between devices  7.3 us (1%)
    another operation x1, loops' own time, per_device(): crossed = lax.fori_loop(0, SWEEPS, advance, crossed)  75.8 us
    mul x64, local copies, waits for them, and re-layouts, column_sweep(): (products * scaled[None, :])[:, :, None] * rolled_v[None, :, :]  71.3 us
    reshape x32, local copies, waits for them, and re-layouts, column_sweep(): rolled = jnp.roll(turned, -offset, axis=1).reshape(width, blocks, BAND)  63.9 us
    sub x32, other arithmetic, column_sweep(): rolled - (products * scaled[None, :])[:, :, None] * rolled_v[None, :, :]  58.7 us
    all_gather x1, blocking collectives, per_device(): whole_v = lax.all_gather(every_sweep, 'rows', axis=1, tiled=True)  51.4 us
    concatenate x32, other arithmetic, column_sweep(): rolled = jnp.roll(turned, -offset, axis=1).reshape(width, blocks, BAND)  50.8 us
    dynamic_slice x64, local copies, waits for them, and re-layouts, advance(): return column_sweep(state, whole_v[sweep_idx], starts[sweep_idx])  48.1 us
    all_to_all x1, blocking collectives, per_device(): lax.all_to_all(crossed.T, 'rows', split_axis=0, concat_axis=1, tiled=True)  25.2 us
  transfers between devices with their start and end apart: 1, of which 0 were waited for; matrix products, arithmetic and copies ran while one was open for 0% of the time, Pallas kernels for 0%

commit v1 on v0

v1 whole, which is shorter than its diff:
```python
import functools
import jax
import jax.numpy as jnp
from jax import lax
from jax.experimental import pallas as pl
from jax.experimental.pallas import tpu as pltpu
from jax.sharding import PartitionSpec as P

BAND = 64
MESH = pl.DeviceIdType.MESH
HIGH = lax.Precision.HIGHEST


def dot(a, b, ca=1, cb=0):
    return lax.dot_general(
        a, b, (((ca,), (cb,)), ((), ())), precision=HIGH, preferred_element_type=jnp.float32
    )


def sweep_ids(shape, axis, sweeps):
    return lax.broadcasted_iota(jnp.int32, shape, axis) % sweeps


def lower(gram, sweeps):
    return jnp.where(sweep_ids(gram.shape, 0, sweeps) > sweep_ids(gram.shape, 1, sweeps), gram, 0.0)


def on_diagonal(shape):
    return lax.broadcasted_iota(jnp.int32, shape, 0) == lax.broadcasted_iota(jnp.int32, shape, 1)


def inverse(full, sweeps, span):
    eye = on_diagonal(full.shape)
    diag = jnp.where(eye, full, 0.0)
    down = jnp.sum(diag, axis=1, keepdims=True)
    across = jnp.sum(diag, axis=0, keepdims=True)
    down = 1.0 / jnp.where(down == 0.0, 1.0, down)
    across = 1.0 / jnp.where(across == 0.0, 1.0, across)
    rows = sweep_ids(full.shape, 0, sweeps)
    cols = sweep_ids(full.shape, 1, sweeps)
    done = jnp.where(eye, down, 0.0)
    size = 1
    while size < span:
        part = (rows // (2 * size) == cols // (2 * size)) & (rows // size > cols // size)
        off = jnp.where(part, full, 0.0)
        if size == 1:
            done = done - down * off * across
        else:
            done = done - dot(done, dot(off, done))
        size *= 2
    return done


def kernel(nrows, ncols, x_hbm, v_ref, starts_ref, out_ref, x_ref, v_all, lt_ref, lt_in, q_send,
           q_near, q_far, p_ref, y_ref, rhs_ref, x_sem, v_local, v_send, v_recv, l_send, l_recv,
           q_send_sem, q_recv_sem):
    d, c = lax.axis_index("rows"), lax.axis_index("cols")
    own = v_ref.shape[0]
    sweeps = v_all.shape[0]
    height, width = x_ref.shape
    depth = height // BAND
    group = 2 * depth
    rounds = sweeps // group
    load = pltpu.make_async_copy(x_hbm, x_ref, x_sem)
    load.start()

    offsets = (-2, -1, 1, 2)

    def there(offset):
        return d + offset >= 0 if offset < 0 else d + offset < nrows

    barrier = pltpu.get_barrier_semaphore()
    for offset in offsets:
        @pl.when(there(offset))
        def _():
            pl.semaphore_signal(barrier, inc=1, device_id=(d + offset, c), device_id_type=MESH)
    for step in range(1, ncols):
        pl.semaphore_signal(barrier, inc=1, device_id=(d, (c + step) % ncols), device_id_type=MESH)
    for i, offset in enumerate(offsets):
        @pl.when(jnp.logical_not(there(offset)))
        def _():
            lt_in[i] = jnp.zeros_like(lt_in[i])
            for r in range(rounds):
                if abs(offset) == 1:
                    q_near[(offset + 1) // 2, r] = jnp.zeros_like(q_near[0, 0])
                else:
                    q_far[(offset + 2) // 4, r] = jnp.zeros_like(q_far[0, 0])
    y_ref[...] = jnp.zeros_like(y_ref)
    rhs_ref[...] = jnp.zeros_like(rhs_ref)
    peers = sum(there(offset).astype(jnp.int32) for offset in offsets)
    pl.semaphore_wait(barrier, peers + (ncols - 1))

    place = v_all.at[pl.ds(pl.multiple_of(c * own, own), own)]
    copies = []
    for step in range(1, ncols):
        copy = pltpu.make_async_remote_copy(
            src_ref=v_ref, dst_ref=place, send_sem=v_send.at[step - 1], recv_sem=v_recv.at[step - 1],
            device_id=(d, (c + step) % ncols), device_id_type=MESH)
        copy.start()
        copies.append(copy)
    mine = pltpu.make_async_copy(v_ref, place, v_local)
    mine.start()
    mine.wait()
    for copy in copies:
        copy.wait()

    v = v_all[...]
    begin = starts_ref[...]
    row = lax.broadcasted_iota(jnp.int32, v.shape, 1)
    window = (row - begin + BAND) // BAND
    outside = ((window == 0) & (d == 0)) | ((window == depth) & (d == nrows - 1) & (begin > 0))
    v = jnp.where(outside, 0.0, v)
    parts = [jnp.where(window == k, v, 0.0) for k in range(depth + 1)]
    u_s = jnp.concatenate([parts[0], parts[depth]], axis=0)
    u_i = jnp.concatenate(parts[1:depth], axis=0)
    half_s = 0.5 * jnp.sum(u_s * u_s, axis=1, keepdims=True)
    half_i = 0.5 * jnp.sum(u_i * u_i, axis=1, keepdims=True)
    g_ii = dot(u_i, u_i, 1, 1)
    n_si = lower(dot(u_s, u_i, 1, 1), sweeps)
    n_is = lower(dot(u_i, u_s, 1, 1), sweeps)
    g_ss = dot(u_s, u_s, 1, 1)
    l_ii = jnp.where(on_diagonal(g_ii.shape), half_i, lower(g_ii, sweeps))
    n_ss = jnp.where(on_diagonal(g_ss.shape), half_s, lower(g_ss, sweeps))
    t = inverse(l_ii, sweeps, sweeps)
    f = dot(t, n_is)
    lt = n_ss - dot(n_si, f)
    lt_ref[...] = lt

    def exchange(i, offset, src, dst, send, recv):
        return pltpu.make_async_remote_copy(
            src_ref=src, dst_ref=dst, send_sem=send, recv_sem=recv,
            device_id=(d + offset, c), device_id_type=MESH)

    def lt_copy(i, offset, slot):
        return exchange(i, offset, lt_ref, lt_in.at[slot], l_send.at[i], l_recv.at[slot])

    def q_copy(i, offset, r, slot):
        if abs(offset) == 1:
            src, dst = q_send.at[r], q_near.at[slot - 1, r]
        else:
            side = 0 if offset < 0 else 1
            src, dst = q_send.at[r, pl.ds(side * group, group)], q_far.at[slot // 3, r]
        return exchange(i, offset, src, dst, q_send_sem.at[i, r], q_recv_sem.at[slot, r])

    for i, offset in enumerate(offsets):
        @pl.when(there(offset))
        def _():
            lt_copy(i, offset, 3 - i).start()

    e = dot(t, u_i)
    b = u_s - dot(n_si, e)
    load.wait()
    x = x_ref[...]
    p_ref[...] = dot(b, x)

    def near_rows(ref, r):
        return jnp.concatenate(
            [ref[pl.ds(group * r, group)], ref[pl.ds(sweeps + group * r, group)]], axis=0)

    def send_round(r):
        q = near_rows(p_ref, r)
        if r > 0:
            q = q - dot(near_rows(lt_ref, r), y_ref[...])
        q_send[r] = q
        for i, offset in enumerate(offsets):
            @pl.when(there(offset))
            def _():
                q_copy(i, offset, r, 3 - i).start()

    send_round(0)
    ct = u_s - dot(f, u_i, 0, 0)
    out_ref[...] = x - dot(u_i, dot(e, x), 0, 0)

    for i, offset in enumerate(offsets):
        @pl.when(there(offset))
        def _():
            lt_copy(i, offset, i).wait_recv()
            lt_copy(i, offset, 3 - i).wait_send()

    def placed(block, at):
        size, total = block.shape[0], 4 * sweeps
        up = (lax.broadcasted_iota(jnp.int32, (total, size), 0)
              == lax.broadcasted_iota(jnp.int32, (total, size), 1) + at)
        up = up.astype(jnp.float32)
        return dot(dot(up, block), up, 1, 1)

    shape = lt.shape
    r_of = lax.broadcasted_iota(jnp.int32, shape, 0) // sweeps
    c_of = lax.broadcasted_iota(jnp.int32, shape, 1) // sweeps
    big = placed(lt_in[1], 0) + placed(lt, sweeps) + placed(lt_in[2], 2 * sweeps)
    big = big + placed(jnp.where((r_of == 1) & (c_of == 1), lt_in[0], 0.0), -sweeps)
    big = big + placed(jnp.where((r_of == 0) & (c_of == 0), lt_in[3], 0.0), 3 * sweeps)
    s = inverse(big, sweeps, group)

    for r in range(rounds):
        for i, offset in enumerate(offsets):
            @pl.when(there(offset))
            def _():
                q_copy(i, offset, r, i).wait_recv()
        at = group * r
        rhs_ref[pl.ds(at, group)] = q_far[0, r] + q_near[0, r, pl.ds(0, group)]
        rhs_ref[pl.ds(sweeps + at, group)] = (
            q_near[0, r, pl.ds(group, group)] + q_send[r, pl.ds(0, group)])
        rhs_ref[pl.ds(2 * sweeps + at, group)] = (
            q_send[r, pl.ds(group, group)] + q_near[1, r, pl.ds(0, group)])
        rhs_ref[pl.ds(3 * sweeps + at, group)] = q_near[1, r, pl.ds(group, group)] + q_far[1, r]
        pick = jnp.concatenate(
            [s[sweeps + at:sweeps + at + group], s[2 * sweeps + at:2 * sweeps + at + group]], axis=0)
        y = dot(pick, rhs_ref[...])
        y_ref[pl.ds(at, group)] = y[:group]
        y_ref[pl.ds(sweeps + at, group)] = y[group:]
        if r + 1 < rounds:
            send_round(r + 1)

    out_ref[...] = out_ref[...] - dot(ct, y_ref[...], 0, 0)
    for r in range(rounds):
        for i, offset in enumerate(offsets):
            @pl.when(there(offset))
            def _():
                q_copy(i, offset, r, 3 - i).wait_send()


def per_device(nrows, ncols, eigvecs, reflectors, starts):
    own, height = reflectors.shape
    width = eigvecs.shape[1]
    sweeps = starts.shape[0]
    group = 2 * (height // BAND)
    rounds = sweeps // group
    f32 = jnp.float32
    return pl.pallas_call(
        functools.partial(kernel, nrows, ncols),
        out_shape=jax.ShapeDtypeStruct((height, width), f32),
        in_specs=[pl.BlockSpec(memory_space=pl.ANY), pl.BlockSpec(memory_space=pltpu.VMEM),
                  pl.BlockSpec(memory_space=pltpu.VMEM)],
        out_specs=pl.BlockSpec(memory_space=pltpu.VMEM),
        scratch_shapes=[
            pltpu.VMEM((height, width), f32),
            pltpu.VMEM((sweeps, height), f32),
            pltpu.VMEM((2 * sweeps, 2 * sweeps), f32),
            pltpu.VMEM((4, 2 * sweeps, 2 * sweeps), f32),
            pltpu.VMEM((rounds, 2 * group, width), f32),
            pltpu.VMEM((2, rounds, 2 * group, width), f32),
            pltpu.VMEM((2, rounds, group, width), f32),
            pltpu.VMEM((2 * sweeps, width), f32),
            pltpu.VMEM((2 * sweeps, width), f32),
            pltpu.VMEM((4 * sweeps, width), f32),
            pltpu.SemaphoreType.DMA,
            pltpu.SemaphoreType.DMA,
            pltpu.SemaphoreType.DMA((ncols - 1,)),
            pltpu.SemaphoreType.DMA((ncols - 1,)),
            pltpu.SemaphoreType.DMA((4,)),
            pltpu.SemaphoreType.DMA((4,)),
            pltpu.SemaphoreType.DMA((4, rounds)),
            pltpu.SemaphoreType.DMA((4, rounds)),
        ],
        compiler_params=pltpu.CompilerParams(collective_id=0, has_side_effects=True),
    )(eigvecs, reflectors, starts.reshape(sweeps, 1))


def solution(mesh):
    in_specs = (P("rows", "cols"), P("cols", "rows"), P())
    out_specs = P("rows", "cols")
    body = functools.partial(per_device, mesh.shape["rows"], mesh.shape["cols"])
    return jax.shard_map(
        body, mesh=mesh, in_specs=in_specs, out_specs=out_specs, check_vma=False
    )
```

time: 532 us -> 37 us (0.07); the launches traced: 526 us -> 36.6 us
  local copies, waits for them, and re-layouts: 190 us -> 3.65 us
  other arithmetic: 174 us -> 0 us
  blocking collectives: 78.4 us -> 0 us
  loops' own time: 75.8 us -> 0 us
  Pallas kernels: 0 us -> 32.9 us
  starting transfers between devices: 7.3 us -> 0 us
    another operation x1 -> x0, loops' own time: 75.8 us -> none  [per_device(): crossed = lax.fori_loop(0, SWEEPS, advance, crossed)]
    mul x96 -> x0, local copies, waits for them, and re-layouts: 73.7 us -> none  [the longest x64 71.3 us: column_sweep(): (products * scaled[None, :])[:, :, None] * rolled_v[None, :, :]]
    concatenate x96 -> x0, other arithmetic: 73.5 us -> none  [the longest x32 50.8 us: column_sweep(): rolled = jnp.roll(turned, -offset, axis=1).reshape(width, blocks, BAND)]
    reshape x32 -> x1, local copies, waits for them, and re-layouts: 63.9 us -> 0.69 us  [per_device(): starts.reshape(sweeps, 1)]
    sub x32 -> x0, other arithmetic: 58.7 us -> none  [column_sweep(): rolled - (products * scaled[None, :])[:, :, None] * rolled_v[None, :, :]]
    all_gather x2 -> x0, blocking collectives: 53.2 us -> none  [the longest x1 51.4 us: per_device(): whole_v = lax.all_gather(every_sweep, 'rows', axis=1, tiled=True)]
    dynamic_slice x64 -> x0, local copies, waits for them, and re-layouts: 48.1 us -> none  [advance(): return column_sweep(state, whole_v[sweep_idx], starts[sweep_idx])]
    pallas_call x0 -> x1, Pallas kernels: none -> 32.9 us  [per_device(): pl.pallas_call(functools.partial(kernel, nrows, ncols), out_shape=jax.Sha...]
  transfers between devices with their start and end apart: 1 -> 0, of which waited for: 0 -> 0; matrix products, arithmetic and copies ran while one was open for 0% -> 0% of each run, Pallas kernels for 0% -> 0%
where the time goes in v1:
time: 37 us; the launch traced here: 36.6 us
  Pallas kernels  32.9 us (89%)
  local copies, waits for them, and re-layouts  3.65 us (10%)
    pallas_call x1, Pallas kernels, per_device(): pl.pallas_call(functools.partial(kernel, nrows, ncols), out_shape=jax.Sha...  32.9 us
    unnamed x3, local copies, waits for them, and re-layouts  2.96 us

profile of v1, /device:TPU:12, one launch (start us, length us, event | category | flops | bytes accessed | tf_op | source)
XLA Modules:
  0.0 36.6 jit_solution(12029744793885802929)
XLA Ops:
  0.0 0.0 copy-start
  0.0 0.7 %copy-done = s32[32]{0:T(128)S(1)} copy-done((s32[32]{0:T(128)S(1)}, s32[32]{0:T(128)}, u32[]{:S(2)}) %copy-start) | copy-done | bytes 152
  0.7 0.7 %copy.4.starts_ref = s32[32,1]{1,0:T(8,128)} copy(s32[32,1]{0,1:T(1,128)S(1)} %bitcast.1) | data formatting | bytes 256 | tf_op jit(solution)/shard_map/reshape | solution.py:257
  1.3 32.9 %shard_map.37 = f32[256,1024]{1,0:T(8,128)} custom-call(f32[256,1024]{1,0:T(8,128)} %x_hbm.1, f32[16,256]{1,0:T(8,128)} %v_ref.1, s32[32,1]{1,0:T(8,128)} %copy.4.starts_ref), custom_call_target="tpu_custom_call" | custom-call | tf_op jit(solution)/shard_map/pallas_call | solution.py:230
  34.3 2.3 %copy.6 = f32[256,1024]{1,0:T(8,128)} copy(f32[256,1024]{1,0:T(8,128)} %shard_map.37) | data formatting | bytes 2097152
Async XLA Ops:
  0.0 0.7 %copy-start = (s32[32]{0:T(128)S(1)}, s32[32]{0:T(128)}, u32[]{:S(2)}) copy-start(s32[32]{0:T(128)} %param.5) | copy-start | bytes 388

commit v2 on v1

--- a/solution.py
+++ b/solution.py
@@ -7,6 +7,7 @@
 from jax.sharding import PartitionSpec as P
 
 BAND = 64
+VMEM_BYTES = 24 * 1024 * 1024
 MESH = pl.DeviceIdType.MESH
 HIGH = lax.Precision.HIGHEST
 
@@ -51,16 +52,21 @@
     return done
 
 
-def kernel(nrows, ncols, x_hbm, v_ref, starts_ref, out_ref, x_ref, v_all, lt_ref, lt_in, q_send,
-           q_near, q_far, p_ref, y_ref, rhs_ref, x_sem, v_local, v_send, v_recv, l_send, l_recv,
-           q_send_sem, q_recv_sem):
+def kernel(nrows, ncols, x_hbm, v_hbm, starts_hbm, ax_ref, ct_ref, y_ref, x_ref, v_all, starts_ref,
+           lt_ref, lt_in, q_own, q_send, q_near, q_far, p_ref, x_sem, s_sem, v_local, v_send, v_recv,
+           l_send, l_recv, q_send_sem, q_recv_sem):
     d, c = lax.axis_index("rows"), lax.axis_index("cols")
-    own = v_ref.shape[0]
+    own = v_hbm.shape[0]
     sweeps = v_all.shape[0]
     height, width = x_ref.shape
     depth = height // BAND
     group = 2 * depth
     rounds = sweeps // group
+    place = v_all.at[pl.ds(pl.multiple_of(c * own, own), own)]
+    mine = pltpu.make_async_copy(v_hbm, place, v_local)
+    mine.start()
+    begins = pltpu.make_async_copy(starts_hbm, starts_ref, s_sem)
+    begins.start()
     load = pltpu.make_async_copy(x_hbm, x_ref, x_sem)
     load.start()
 
@@ -80,32 +86,28 @@
         @pl.when(jnp.logical_not(there(offset)))
         def _():
             lt_in[i] = jnp.zeros_like(lt_in[i])
-            for r in range(rounds):
-                if abs(offset) == 1:
-                    q_near[(offset + 1) // 2, r] = jnp.zeros_like(q_near[0, 0])
-                else:
-                    q_far[(offset + 2) // 4, r] = jnp.zeros_like(q_far[0, 0])
+            if abs(offset) == 1:
+                q_near[i - 1] = jnp.zeros_like(q_near[0])
+            else:
+                q_far[i // 3] = jnp.zeros_like(q_far[0])
     y_ref[...] = jnp.zeros_like(y_ref)
-    rhs_ref[...] = jnp.zeros_like(rhs_ref)
     peers = sum(there(offset).astype(jnp.int32) for offset in offsets)
     pl.semaphore_wait(barrier, peers + (ncols - 1))
 
-    place = v_all.at[pl.ds(pl.multiple_of(c * own, own), own)]
+    mine.wait()
     copies = []
     for step in range(1, ncols):
         copy = pltpu.make_async_remote_copy(
-            src_ref=v_ref, dst_ref=place, send_sem=v_send.at[step - 1], recv_sem=v_recv.at[step - 1],
+            src_ref=place, dst_ref=place, send_sem=v_send.at[step - 1], recv_sem=v_recv.at[step - 1],
             device_id=(d, (c + step) % ncols), device_id_type=MESH)
         copy.start()
         copies.append(copy)
-    mine = pltpu.make_async_copy(v_ref, place, v_local)
-    mine.start()
-    mine.wait()
+    begins.wait()
+    across = jnp.broadcast_to(starts_ref[...], (sweeps, sweeps))
+    begin = jnp.sum(jnp.where(on_diagonal(across.shape), across, 0), axis=1, keepdims=True)
     for copy in copies:
         copy.wait()
-
     v = v_all[...]
-    begin = starts_ref[...]
     row = lax.broadcasted_iota(jnp.int32, v.shape, 1)
     window = (row - begin + BAND) // BAND
     outside = ((window == 0) & (d == 0)) | ((window == depth) & (d == nrows - 1) & (begin > 0))
@@ -135,11 +137,11 @@
         return exchange(i, offset, lt_ref, lt_in.at[slot], l_send.at[i], l_recv.at[slot])
 
     def q_copy(i, offset, r, slot):
+        side = 0 if offset < 0 else 1
         if abs(offset) == 1:
-            src, dst = q_send.at[r], q_near.at[slot - 1, r]
+            src, dst = q_send.at[side, r], q_near.at[slot - 1, r]
         else:
-            side = 0 if offset < 0 else 1
-            src, dst = q_send.at[r, pl.ds(side * group, group)], q_far.at[slot // 3, r]
+            src, dst = q_send.at[side, r, 0], q_far.at[slot // 3, r]
         return exchange(i, offset, src, dst, q_send_sem.at[i, r], q_recv_sem.at[slot, r])
 
     for i, offset in enumerate(offsets):
@@ -161,7 +163,11 @@
         q = near_rows(p_ref, r)
         if r > 0:
             q = q - dot(near_rows(lt_ref, r), y_ref[...])
-        q_send[r] = q
+        q_own[r] = q
+        for side in range(2):
+            for part in range(2):
+                q_send[side, r, part] = q[side * group + part * depth:side * group + (part + 1) * depth]
+            q_send[side, r, 2] = q[(1 - side) * group:(1 - side) * group + depth]
         for i, offset in enumerate(offsets):
             @pl.when(there(offset))
             def _():
@@ -169,7 +175,8 @@
 
     send_round(0)
     ct = u_s - dot(f, u_i, 0, 0)
-    out_ref[...] = x - dot(u_i, dot(e, x), 0, 0)
+    ax_ref[...] = x - dot(u_i, dot(e, x), 0, 0)
+    ct_ref[...] = ct
 
     for i, offset in enumerate(offsets):
         @pl.when(there(offset))
@@ -192,32 +199,48 @@
     big = big + placed(jnp.where((r_of == 0) & (c_of == 0), lt_in[3], 0.0), 3 * sweeps)
     s = inverse(big, sweeps, group)
 
+    compact = []
+    for r in range(rounds):
+        at = group * r
+        pick = jnp.concatenate(
+            [s[sweeps + at:sweeps + at + group], s[2 * sweeps + at:2 * sweeps + at + group]], axis=0)
+        from_col = lax.broadcasted_iota(jnp.int32, (4 * sweeps, 4 * group), 0)
+        to_col = lax.broadcasted_iota(jnp.int32, (4 * sweeps, 4 * group), 1)
+        same = from_col == to_col // group * sweeps + at + to_col % group
+        compact.append(dot(pick, same.astype(jnp.float32)))
+
     for r in range(rounds):
         for i, offset in enumerate(offsets):
             @pl.when(there(offset))
             def _():
                 q_copy(i, offset, r, i).wait_recv()
         at = group * r
-        rhs_ref[pl.ds(at, group)] = q_far[0, r] + q_near[0, r, pl.ds(0, group)]
-        rhs_ref[pl.ds(sweeps + at, group)] = (
-            q_near[0, r, pl.ds(group, group)] + q_send[r, pl.ds(0, group)])
-        rhs_ref[pl.ds(2 * sweeps + at, group)] = (
-            q_send[r, pl.ds(group, group)] + q_near[1, r, pl.ds(0, group)])
-        rhs_ref[pl.ds(3 * sweeps + at, group)] = q_near[1, r, pl.ds(group, group)] + q_far[1, r]
-        pick = jnp.concatenate(
-            [s[sweeps + at:sweeps + at + group], s[2 * sweeps + at:2 * sweeps + at + group]], axis=0)
-        y = dot(pick, rhs_ref[...])
+        zero = jnp.zeros((depth, width), jnp.float32)
+        rhs = jnp.concatenate([
+            q_far[0, r] + q_near[0, r, 2],
+            zero,
+            q_near[0, r, 0] + q_own[r, pl.ds(0, depth)],
+            q_near[0, r, 1] + q_own[r, pl.ds(depth, depth)],
+            q_near[1, r, 0] + q_own[r, pl.ds(group, depth)],
+            q_near[1, r, 1] + q_own[r, pl.ds(group + depth, depth)],
+            q_near[1, r, 2] + q_far[1, r],
+            zero,
+        ], axis=0)
+        y = dot(compact[r], rhs)
         y_ref[pl.ds(at, group)] = y[:group]
         y_ref[pl.ds(sweeps + at, group)] = y[group:]
         if r + 1 < rounds:
             send_round(r + 1)
 
-    out_ref[...] = out_ref[...] - dot(ct, y_ref[...], 0, 0)
     for r in range(rounds):
         for i, offset in enumerate(offsets):
             @pl.when(there(offset))
             def _():
                 q_copy(i, offset, r, 3 - i).wait_send()
+
+
+def finish(ax_ref, ct_ref, y_ref, out_ref):
+    out_ref[...] = ax_ref[...] - dot(ct_ref[...], y_ref[...], 0, 0)
 
 
 def per_device(nrows, ncols, eigvecs, reflectors, starts):
@@ -227,23 +250,27 @@
     group = 2 * (height // BAND)
     rounds = sweeps // group
     f32 = jnp.float32
-    return pl.pallas_call(
+    vmem = pl.BlockSpec(memory_space=pltpu.VMEM)
+    hbm = pl.BlockSpec(memory_space=pltpu.HBM)
+    ax, ct, y = pl.pallas_call(
         functools.partial(kernel, nrows, ncols),
-        out_shape=jax.ShapeDtypeStruct((height, width), f32),
-        in_specs=[pl.BlockSpec(memory_space=pl.ANY), pl.BlockSpec(memory_space=pltpu.VMEM),
-                  pl.BlockSpec(memory_space=pltpu.VMEM)],
-        out_specs=pl.BlockSpec(memory_space=pltpu.VMEM),
+        out_shape=(jax.ShapeDtypeStruct((height, width), f32),
+                   jax.ShapeDtypeStruct((2 * sweeps, height), f32),
+                   jax.ShapeDtypeStruct((2 * sweeps, width), f32)),
+        in_specs=[hbm, hbm, hbm],
+        out_specs=(vmem, vmem, vmem),
         scratch_shapes=[
             pltpu.VMEM((height, width), f32),
             pltpu.VMEM((sweeps, height), f32),
+            pltpu.VMEM((1, sweeps), jnp.int32),
             pltpu.VMEM((2 * sweeps, 2 * sweeps), f32),
             pltpu.VMEM((4, 2 * sweeps, 2 * sweeps), f32),
             pltpu.VMEM((rounds, 2 * group, width), f32),
-            pltpu.VMEM((2, rounds, 2 * group, width), f32),
-            pltpu.VMEM((2, rounds, group, width), f32),
+            pltpu.VMEM((2, rounds, 3, group // 2, width), f32),
+            pltpu.VMEM((2, rounds, 3, group // 2, width), f32),
+            pltpu.VMEM((2, rounds, group // 2, width), f32),
             pltpu.VMEM((2 * sweeps, width), f32),
-            pltpu.VMEM((2 * sweeps, width), f32),
-            pltpu.VMEM((4 * sweeps, width), f32),
+            pltpu.SemaphoreType.DMA,
             pltpu.SemaphoreType.DMA,
             pltpu.SemaphoreType.DMA,
             pltpu.SemaphoreType.DMA((ncols - 1,)),
@@ -253,8 +280,20 @@
             pltpu.SemaphoreType.DMA((4, rounds)),
             pltpu.SemaphoreType.DMA((4, rounds)),
         ],
-        compiler_params=pltpu.CompilerParams(collective_id=0, has_side_effects=True),
-    )(eigvecs, reflectors, starts.reshape(sweeps, 1))
+        compiler_params=pltpu.CompilerParams(
+            collective_id=0, has_side_effects=True, vmem_limit_bytes=VMEM_BYTES),
+    )(eigvecs, reflectors, starts.reshape(1, sweeps))
+    tile = width // 4
+    return pl.pallas_call(
+        finish,
+        grid=(width // tile,),
+        out_shape=jax.ShapeDtypeStruct((height, width), f32),
+        in_specs=[pl.BlockSpec((height, tile), lambda i: (0, i)),
+                  pl.BlockSpec((2 * sweeps, height), lambda i: (0, 0)),
+                  pl.BlockSpec((2 * sweeps, tile), lambda i: (0, i))],
+        out_specs=pl.BlockSpec((height, tile), lambda i: (0, i)),
+        compiler_params=pltpu.CompilerParams(vmem_limit_bytes=VMEM_BYTES),
+    )(ax, ct, y)
 
 
 def solution(mesh):

time: 37 us -> 33.5 us (0.905)
  Pallas kernels: 32.9 us -> 30.4 us
  local copies, waits for them, and re-layouts: 3.65 us -> 2.6 us
    pallas_call x1 -> x2, Pallas kernels: 32.9 us -> 30.4 us  [the longest x1 27.7 us: per_device(): pl.pallas_call(functools.partial(kernel, nrows, ncols), out_shape=(jax.Sh...]
    reshape x1 -> x0, local copies, waits for them, and re-layouts: 0.69 us -> none  [per_device(): starts.reshape(sweeps, 1)]
    unnamed x3 -> x6, local copies, waits for them, and re-layouts: 2.96 us -> 2.6 us
where the time goes in v2:
time: 33.5 us; the launch traced here: 33 us
  Pallas kernels  30.4 us (91%)
  local copies, waits for them, and re-layouts  2.6 us (8%)
    pallas_call x1, Pallas kernels, per_device(): pl.pallas_call(functools.partial(kernel, nrows, ncols), out_shape=(jax.Sh...  27.7 us
    pallas_call x1, Pallas kernels, per_device(): pl.pallas_call(finish, grid=(width // tile,), out_shape=jax.ShapeDtypeStr...  2.78 us
    unnamed x6, local copies, waits for them, and re-layouts  2.6 us

profile of v2, /device:TPU:12, one launch (start us, length us, event | category | flops | bytes accessed | tf_op | source)
XLA Modules:
  0.0 33.0 jit_solution(12703732787355748704)
XLA Ops:
  0.0 0.0 copy-start.2
  0.0 0.7 %copy-done.2 = s32[32]{0:T(128)S(1)} copy-done((s32[32]{0:T(128)S(1)}, s32[32]{0:T(128)}, u32[]{:S(2)}) %copy-start.2) | copy-done | bytes 152
  0.7 0.0 copy-start
  0.7 1.2 %copy-done = f32[256,1024]{1,0:T(8,128)S(1)} copy-done((f32[256,1024]{1,0:T(8,128)S(1)}, f32[256,1024]{1,0:T(8,128)}, u32[]{:S(2)}) %copy-start) | copy-done | bytes 1048600
  1.9 0.0 copy-start.1
  1.9 0.7 %copy-done.1 = f32[16,256]{1,0:T(8,128)S(1)} copy-done((f32[16,256]{1,0:T(8,128)S(1)}, f32[16,256]{1,0:T(8,128)}, u32[]{:S(2)}) %copy-start.1) | copy-done | bytes 16408
  2.6 27.7 %shard_map.37 = (f32[256,1024]{1,0:T(8,128)S(1)}, f32[64,256]{1,0:T(8,128)S(1)}, f32[64,1024]{1,0:T(8,128)S(1)}) custom-call(f32[256,1024]{1,0:T(8,128)S(1)} %copy-done, f32[16,256]{1,0:T(8,128)S(1)} %copy-done.1, s32[1,32]{1,0:T(1,128)S(1)} %bitcast.1), custom_call_target="tpu_custom_call" | custom-call | tf_op jit(solution)/shard_map/pallas_call | solution.py:255
  30.3 2.8 %shard_map.38 = f32[256,1024]{1,0:T(8,128)} custom-call(f32[256,1024]{1,0:T(8,128)S(1)} %get-tuple-element.8.ax_ref, f32[64,256]{1,0:T(8,128)S(1)} %get-tuple-element.9.ct_ref, f32[64,1024]{1,0:T(8,128)S(1)} %get-tuple-element.10.y_ref), custom_call_target="tpu_custom_call" | custom-call | tf_op jit(solution)/shard_map/pallas_call | solution.py:287
Async XLA Ops:
  0.0 0.7 %copy-start.2 = (s32[32]{0:T(128)S(1)}, s32[32]{0:T(128)}, u32[]{:S(2)}) copy-start(s32[32]{0:T(128)} %param.5) | copy-start | bytes 388
  0.7 1.2 %copy-start = (f32[256,1024]{1,0:T(8,128)S(1)}, f32[256,1024]{1,0:T(8,128)}, u32[]{:S(2)}) copy-start(f32[256,1024]{1,0:T(8,128)} %x_hbm.1) | copy-start | bytes 3145732
  1.9 0.7 %copy-start.1 = (f32[16,256]{1,0:T(8,128)S(1)}, f32[16,256]{1,0:T(8,128)}, u32[]{:S(2)}) copy-start(f32[16,256]{1,0:T(8,128)} %v_hbm.1) | copy-start | bytes 49156

commit v3 on v2

--- a/solution.py
+++ b/solution.py
@@ -7,7 +7,6 @@
 from jax.sharding import PartitionSpec as P
 
 BAND = 64
-VMEM_BYTES = 24 * 1024 * 1024
 MESH = pl.DeviceIdType.MESH
 HIGH = lax.Precision.HIGHEST
 
@@ -16,6 +15,18 @@
     return lax.dot_general(
         a, b, (((ca,), (cb,)), ((), ())), precision=HIGH, preferred_element_type=jnp.float32
     )
+
+
+def halves(a):
+    high = a.astype(jnp.bfloat16)
+    return high, (a - high.astype(jnp.float32)).astype(jnp.bfloat16)
+
+
+def dot_split(a, b, ca=1, cb=0):
+    def one(left, right):
+        return lax.dot_general(
+            left, right, (((ca,), (cb,)), ((), ())), preferred_element_type=jnp.float32)
+    return one(a[0], b[0]) + (one(a[0], b[1]) + one(a[1], b[0]))
 
 
 def sweep_ids(shape, axis, sweeps):
@@ -52,9 +63,9 @@
     return done
 
 
-def kernel(nrows, ncols, x_hbm, v_hbm, starts_hbm, ax_ref, ct_ref, y_ref, x_ref, v_all, starts_ref,
+def kernel(nrows, ncols, x_hbm, v_hbm, starts_hbm, ax_hbm, cm_hbm, y_hbm, x_ref, v_all, starts_ref,
            lt_ref, lt_in, q_own, q_send, q_near, q_far, p_ref, x_sem, s_sem, v_local, v_send, v_recv,
-           l_send, l_recv, q_send_sem, q_recv_sem):
+           l_send, l_recv, q_send_sem, q_recv_sem, ax_ref, cm_ref, y_ref, out_sem, y_sem):
     d, c = lax.axis_index("rows"), lax.axis_index("cols")
     own = v_hbm.shape[0]
     sweeps = v_all.shape[0]
@@ -152,8 +163,8 @@
     e = dot(t, u_i)
     b = u_s - dot(n_si, e)
     load.wait()
-    x = x_ref[...]
-    p_ref[...] = dot(b, x)
+    x_halves = halves(x_ref[...])
+    p_ref[...] = dot_split(halves(b), x_halves)
 
     def near_rows(ref, r):
         return jnp.concatenate(
@@ -174,9 +185,14 @@
                 q_copy(i, offset, r, 3 - i).start()
 
     send_round(0)
-    ct = u_s - dot(f, u_i, 0, 0)
-    ax_ref[...] = x - dot(u_i, dot(e, x), 0, 0)
-    ct_ref[...] = ct
+    u_t = u_i.T
+    cm_ref[...] = u_s.T - dot(u_t, f)
+    inner = dot_split(halves(e), x_halves)
+    ax_ref[...] = x_ref[...] - dot_split(halves(u_t), halves(inner))
+    outs = [pltpu.make_async_copy(ax_ref, ax_hbm, out_sem.at[0]),
+            pltpu.make_async_copy(cm_ref, cm_hbm, out_sem.at[1])]
+    for out in outs:
+        out.start()
 
     for i, offset in enumerate(offsets):
         @pl.when(there(offset))
@@ -231,16 +247,22 @@
         y_ref[pl.ds(sweeps + at, group)] = y[group:]
         if r + 1 < rounds:
             send_round(r + 1)
+        for side in range(2):
+            rows = pl.ds(side * sweeps + at, group)
+            outs.append(pltpu.make_async_copy(y_ref.at[rows], y_hbm.at[rows], y_sem.at[side, r]))
+            outs[-1].start()
 
     for r in range(rounds):
         for i, offset in enumerate(offsets):
             @pl.when(there(offset))
             def _():
                 q_copy(i, offset, r, 3 - i).wait_send()
-
-
-def finish(ax_ref, ct_ref, y_ref, out_ref):
-    out_ref[...] = ax_ref[...] - dot(ct_ref[...], y_ref[...], 0, 0)
+    for out in outs:
+        out.wait()
+
+
+def finish(ax_ref, cm_ref, y_ref, out_ref):
+    out_ref[...] = ax_ref[...] - dot_split(halves(cm_ref[...]), halves(y_ref[...]))
 
 
 def per_device(nrows, ncols, eigvecs, reflectors, starts):
@@ -250,15 +272,14 @@
     group = 2 * (height // BAND)
     rounds = sweeps // group
     f32 = jnp.float32
-    vmem = pl.BlockSpec(memory_space=pltpu.VMEM)
-    hbm = pl.BlockSpec(memory_space=pltpu.HBM)
-    ax, ct, y = pl.pallas_call(
+    hbm = pl.BlockSpec(memory_space=pl.ANY)
+    ax, cm, y = pl.pallas_call(
         functools.partial(kernel, nrows, ncols),
         out_shape=(jax.ShapeDtypeStruct((height, width), f32),
-                   jax.ShapeDtypeStruct((2 * sweeps, height), f32),
+                   jax.ShapeDtypeStruct((height, 2 * sweeps), f32),
                    jax.ShapeDtypeStruct((2 * sweeps, width), f32)),
         in_specs=[hbm, hbm, hbm],
-        out_specs=(vmem, vmem, vmem),
+        out_specs=(hbm, hbm, hbm),
         scratch_shapes=[
             pltpu.VMEM((height, width), f32),
             pltpu.VMEM((sweeps, height), f32),
@@ -279,9 +300,14 @@
             pltpu.SemaphoreType.DMA((4,)),
             pltpu.SemaphoreType.DMA((4, rounds)),
             pltpu.SemaphoreType.DMA((4, rounds)),
+            pltpu.VMEM((height, width), f32),
+            pltpu.VMEM((height, 2 * sweeps), f32),
+            pltpu.VMEM((2 * sweeps, width), f32),
+            pltpu.SemaphoreType.DMA((2,)),
+            pltpu.SemaphoreType.DMA((2, rounds)),
         ],
         compiler_params=pltpu.CompilerParams(
-            collective_id=0, has_side_effects=True, vmem_limit_bytes=VMEM_BYTES),
+            collective_id=0, has_side_effects=True),
     )(eigvecs, reflectors, starts.reshape(1, sweeps))
     tile = width // 4
     return pl.pallas_call(
@@ -289,11 +315,10 @@
         grid=(width // tile,),
         out_shape=jax.ShapeDtypeStruct((height, width), f32),
         in_specs=[pl.BlockSpec((height, tile), lambda i: (0, i)),
-                  pl.BlockSpec((2 * sweeps, height), lambda i: (0, 0)),
+                  pl.BlockSpec((height, 2 * sweeps), lambda i: (0, 0)),
                   pl.BlockSpec((2 * sweeps, tile), lambda i: (0, i))],
         out_specs=pl.BlockSpec((height, tile), lambda i: (0, i)),
-        compiler_params=pltpu.CompilerParams(vmem_limit_bytes=VMEM_BYTES),
-    )(ax, ct, y)
+    )(ax, cm, y)
 
 
 def solution(mesh):

time: 33.5 us -> 32.7 us (0.976)
  local copies, waits for them, and re-layouts: 2.6 us -> 0 us
  Pallas kernels: 30.4 us -> 32.4 us
    unnamed x6 -> x0, local copies, waits for them, and re-layouts: 2.6 us -> none
    pallas_call x1, Pallas kernels: 2.78 us -> 3.9 us  [per_device(): pl.pallas_call(finish, grid=(width // tile,), out_shape=jax.ShapeDtypeStr...]
    pallas_call x1, Pallas kernels: 27.7 us -> 28.5 us  [per_device(): pl.pallas_call(functools.partial(kernel, nrows, ncols), out_shape=(jax.Sh...]
where the time goes in v3:
time: 32.7 us; the launch traced here: 32.4 us
  Pallas kernels  32.4 us (99%)
    pallas_call x1, Pallas kernels, per_device(): pl.pallas_call(functools.partial(kernel, nrows, ncols), out_shape=(jax.Sh...  28.5 us
    pallas_call x1, Pallas kernels, per_device(): pl.pallas_call(finish, grid=(width // tile,), out_shape=jax.ShapeDtypeStr...  3.9 us

profile of v3, /device:TPU:12, one launch (start us, length us, event | category | flops | bytes accessed | tf_op | source)
XLA Modules:
  0.0 32.4 jit_solution(14922174841767851032)
XLA Ops:
  0.0 28.5 %shard_map.37 = (f32[256,1024]{1,0:T(8,128)}, f32[256,64]{1,0:T(8,128)}, f32[64,1024]{1,0:T(8,128)}) custom-call(f32[256,1024]{1,0:T(8,128)} %x_hbm.1, f32[16,256]{1,0:T(8,128)} %v_hbm.1, s32[1,32]{1,0:T(1,128)} %bitcast.1), custom_call_target="tpu_custom_call" | custom-call | tf_op jit(solution)/shard_map/pallas_call | solution.py:276
  28.5 3.9 %shard_map.38 = f32[256,1024]{1,0:T(8,128)} custom-call(f32[256,1024]{1,0:T(8,128)} %get-tuple-element.8.ax_ref, f32[256,64]{1,0:T(8,128)} %get-tuple-element.9.cm_ref, f32[64,1024]{1,0:T(8,128)} %get-tuple-element.10.y_ref), custom_call_target="tpu_custom_call" | custom-call | tf_op jit(solution)/shard_map/pallas_call | solution.py:313

commit v4 on v3

--- a/solution.py
+++ b/solution.py
@@ -173,7 +173,7 @@
     def send_round(r):
         q = near_rows(p_ref, r)
         if r > 0:
-            q = q - dot(near_rows(lt_ref, r), y_ref[...])
+            q = q - dot_split(halves(near_rows(lt_ref, r)), halves(y_ref[...]))
         q_own[r] = q
         for side in range(2):
             for part in range(2):
@@ -223,7 +223,7 @@
         from_col = lax.broadcasted_iota(jnp.int32, (4 * sweeps, 4 * group), 0)
         to_col = lax.broadcasted_iota(jnp.int32, (4 * sweeps, 4 * group), 1)
         same = from_col == to_col // group * sweeps + at + to_col % group
-        compact.append(dot(pick, same.astype(jnp.float32)))
+        compact.append(halves(dot(pick, same.astype(jnp.float32))))
 
     for r in range(rounds):
         for i, offset in enumerate(offsets):
@@ -242,7 +242,7 @@
             q_near[1, r, 2] + q_far[1, r],
             zero,
         ], axis=0)
-        y = dot(compact[r], rhs)
+        y = dot_split(compact[r], halves(rhs))
         y_ref[pl.ds(at, group)] = y[:group]
         y_ref[pl.ds(sweeps + at, group)] = y[group:]
         if r + 1 < rounds:
@@ -309,7 +309,7 @@
         compiler_params=pltpu.CompilerParams(
             collective_id=0, has_side_effects=True),
     )(eigvecs, reflectors, starts.reshape(1, sweeps))
-    tile = width // 4
+    tile = width // 2
     return pl.pallas_call(
         finish,
         grid=(width // tile,),

time: 32.7 us -> 31.2 us (0.954)
  Pallas kernels: 32.4 us -> 31 us
    pallas_call x1, Pallas kernels: 3.9 us -> 2.63 us  [per_device(): pl.pallas_call(finish, grid=(width // tile,), out_shape=jax.ShapeDtypeStr...]
where the time goes in v4:
time: 31.2 us; the launch traced here: 31 us
  Pallas kernels  31 us (99%)
    pallas_call x1, Pallas kernels, per_device(): pl.pallas_call(functools.partial(kernel, nrows, ncols), out_shape=(jax.Sh...  28.4 us
    pallas_call x1, Pallas kernels, per_device(): pl.pallas_call(finish, grid=(width // tile,), out_shape=jax.ShapeDtypeStr...  2.63 us

profile of v4, /device:TPU:12, one launch (start us, length us, event | category | flops | bytes accessed | tf_op | source)
XLA Modules:
  0.0 31.0 jit_solution(10691092074769122189)
XLA Ops:
  0.0 28.4 %shard_map.37 = (f32[256,1024]{1,0:T(8,128)}, f32[256,64]{1,0:T(8,128)}, f32[64,1024]{1,0:T(8,128)}) custom-call(f32[256,1024]{1,0:T(8,128)} %x_hbm.1, f32[16,256]{1,0:T(8,128)} %v_hbm.1, s32[1,32]{1,0:T(1,128)} %bitcast.1), custom_call_target="tpu_custom_call" | custom-call | tf_op jit(solution)/shard_map/pallas_call | solution.py:276
  28.4 2.6 %shard_map.38 = f32[256,1024]{1,0:T(8,128)} custom-call(f32[256,1024]{1,0:T(8,128)} %get-tuple-element.8.ax_ref, f32[256,64]{1,0:T(8,128)} %get-tuple-element.9.cm_ref, f32[64,1024]{1,0:T(8,128)} %get-tuple-element.10.y_ref), custom_call_target="tpu_custom_call" | custom-call | tf_op jit(solution)/shard_map/pallas_call | solution.py:313
